TPU v7x, 128 devices: a whole 4x4x4 slice. The times are simulated.
128 devices in a mesh: img: 8 (over x, core), slab: 16 (over z, y).
Axes of the slice: x: 4, y: 4, z: 4, core: 2. Of those that a mesh axis runs over, the one named last changes fastest.
Arguments:
- section_input: bfloat16 [1024, 256, 1024], P(('img', 'slab')), parts along dimension 0, may hold values from -54 to 54
- w_reduce: bfloat16 [3, 1024, 256], replicated, may hold values from -0.1875 to 0.1875
- w_spatial: bfloat16 [3, 9, 256, 256], replicated, may hold values from -0.125 to 0.125
- w_expand: bfloat16 [3, 256, 1024], replicated, may hold values from -0.375 to 0.375
- gain_mid: float32 [3, 2, 256], replicated, may hold values from 0.25 to 1.75
- shift_mid: float32 [3, 2, 256], replicated, may hold values from -3 to 3
- gain_out: float32 [3, 1024], replicated, may hold values from 0.25 to 1.75
- shift_out: float32 [3, 1024], replicated, may hold values from -3 to 3
Outputs:
- section_output: bfloat16 [1024, 256, 1024], P(('img', 'slab')), parts along dimension 0
There are 8 independent parts, one for each index of `img`. A program takes and returns all parts, laid end to end along the dimension named above; an argument that names none is the same for every part. Nothing has to cross between parts.
All inputs are finite; a program needn't handle non-finite values.
Results may differ from a plain program's by a relative error of at most 0.01.
Values may be sent and summed in bfloat16 or wider, within the bound.
A program may use at most 128 MiB of HBM per device.

v0:
```python
import jax
import jax.numpy as jnp
from jax import lax
from jax.sharding import PartitionSpec as P


def sent_to_all(x, axis):
    length = lax.axis_size(axis)
    return lax.all_to_all(jnp.broadcast_to(x[None], (length, *x.shape)), axis, 0, 0, tiled=True)


def of_everyone(x, axis):
    everything = sent_to_all(x, axis)
    return jnp.sum(everything, axis=0)


def together(arrays, axis):
    vector, at, finished = (jnp.concatenate([a.reshape(-1) for a in arrays]), 0, [])
    so_far = of_everyone(vector, axis)
    for a in arrays:
        finished.append(so_far[at : at + a.size].reshape(a.shape))
        at += a.size
    return tuple(finished)


def with_halo(block, sides, width):
    for axis, dim in sides:
        count = lax.axis_size(axis)
        forward = [(i, i + 1) for i in range(count - 1)]
        backward = [(target, source) for source, target in forward]
        low = lax.ppermute(
            lax.slice_in_dim(block, block.shape[dim] - width, None, axis=dim), axis, forward
        )
        high = lax.ppermute(lax.slice_in_dim(block, 0, width, axis=dim), axis, backward)
        block = jnp.concatenate([low, block, high], axis=dim)
    return block


def batch_stats(values, count):
    total, squares = together((jnp.sum(values, axis=0), jnp.sum(values * values, axis=0)), "slab")
    mean = total / count
    var = jnp.maximum(squares / count - mean * mean, 0.0)
    return (mean, lax.rsqrt(var + 1e-05))


def spatial_conv(padded_rows, taps, rows, width):
    mid = padded_rows.shape[2]
    padded = jnp.pad(padded_rows, ((0, 0), (1, 1), (0, 0)))
    total = jnp.zeros((rows * width, taps.shape[2]), jnp.float32)
    for down in range(3):
        for across in range(3):
            window = padded[down : down + rows, across : across + width].reshape(-1, mid)
            total = total + jnp.dot(
                window, taps[3 * down + across], preferred_element_type=jnp.float32
            )
    return total


def local(section_input, w_reduce, w_spatial, w_expand, gain_mid, shift_mid, gain_out, shift_out):
    rows, width, chans = section_input.shape
    mid = w_reduce.shape[2]
    slabs = lax.axis_size("slab")
    count = float(rows * width * slabs)
    current = section_input
    for layer in range(w_reduce.shape[0]):
        flat = current.reshape(-1, chans)
        gain_one = gain_mid[layer, 0]
        shift_one = shift_mid[layer, 0]
        reduced = jnp.dot(flat, w_reduce[layer], preferred_element_type=jnp.float32)
        mean, scale = batch_stats(reduced, count)
        hidden = jnp.maximum((reduced - mean) * scale * gain_one + shift_one, 0.0).astype(
            jnp.bfloat16
        )
        padded_rows = with_halo(hidden.reshape(rows, width, mid), (("slab", 0),), 1)
        spatial = spatial_conv(padded_rows, w_spatial[layer], rows, width)
        mean, scale = batch_stats(spatial, count)
        inner = jnp.maximum(
            (spatial - mean) * scale * gain_mid[layer, 1] + shift_mid[layer, 1], 0.0
        ).astype(jnp.bfloat16)
        expanded = jnp.dot(inner, w_expand[layer], preferred_element_type=jnp.float32)
        mean, scale = batch_stats(expanded, count)
        summed = (
            (expanded - mean) * scale * gain_out[layer]
            + shift_out[layer]
            + flat.astype(jnp.float32)
        )
        current = jnp.maximum(summed, 0.0).astype(jnp.bfloat16).reshape(rows, width, chans)
    return current


def solution(mesh):
    placed = (P(("img", "slab"), None, None), P(), P(), P(), P(), P(), P(), P())
    return jax.shard_map(
        local, mesh=mesh, in_specs=placed, out_specs=P(("img", "slab"), None, None), check_vma=False
    )
```

profile of v0, /device:TPU:0, one launch (start us, length us, event | category | flops | bytes accessed | tf_op | source)
XLA Modules:
  0.0 229.2 jit_solution(13923929323437798494)
XLA Ops:
  0.0 3.6 %fusion.130 = (f32[256]{0:T(256)S(1)}, f32[256]{0:T(256)S(1)}, f32[2048,256]{1,0:T(8,128)S(1)}) fusion(bf16[2048,1024]{1,0:T(8,128)(2,1)} %bitcast.213, bf16[3,1024,256]{2,1,0:T(8,128)(2,1)} %param.9), kind=kOutput, calls=%fused_computation.212 | convolution fusion | flops 1075314176 | bytes 6817792 | tf_op jit(solution)/shard_map/dot_general | solution.py:69
  4.2 8.2 %all-to-all-start = ((f32[16,1,512]{2,1,0:T(1,128)}), f32[16,1,512]{2,1,0:T(1,128)S(1)}, u32[]{:S(2)}, u32[]{:S(2)}) async-start(f32[16,1,512]{2,1,0:T(1,128)} %broadcast_in_dim.18), calls=%async_computation | async-start | bytes 65536 | tf_op jit(solution)/shard_map/all_to_all | solution.py:9
  13.6 6.4 %all-to-all-done = f32[16,1,512]{2,1,0:T(1,128)S(1)} async-done(((f32[16,1,512]{2,1,0:T(1,128)}), f32[16,1,512]{2,1,0:T(1,128)S(1)}, u32[]{:S(2)}, u32[]{:S(2)}) %all-to-all-start) | async-done | bytes 32800 | tf_op jit(solution)/shard_map/all_to_all | solution.py:9
  25.5 4.4 %collective-permute-done.1 = bf16[1,256,256]{2,1,0:T(8,128)(2,1)S(1)} collective-permute-done((bf16[1,256,256]{2,1,0:T(8,128)(2,1)S(1)}, bf16[1,256,256]{2,1,0:T(8,128)(2,1)S(1)}, u32[]{:S(2)}, u32[]{:S(2)}) %collective-permute-start.1) | collective-permute-done | bytes 131104 | tf_op jit(solution)/shard_map/ppermute | solution.py:34
  38.4 7.7 %all-to-all-start.1 = ((f32[16,1,512]{2,1,0:T(1,128)}), f32[16,1,512]{2,1,0:T(1,128)}, u32[]{:S(2)}, u32[]{:S(2)}) async-start(f32[16,1,512]{2,1,0:T(1,128)} %broadcast_in_dim.19), calls=%async_computation.1 | async-start | bytes 65536 | tf_op jit(solution)/shard_map/all_to_all | solution.py:9
  47.6 6.2 %all-to-all-done.1 = f32[16,1,512]{2,1,0:T(1,128)} async-done(((f32[16,1,512]{2,1,0:T(1,128)}), f32[16,1,512]{2,1,0:T(1,128)}, u32[]{:S(2)}, u32[]{:S(2)}) %all-to-all-start.1) | async-done | bytes 32800 | tf_op jit(solution)/shard_map/all_to_all | solution.py:9
  54.6 6.4 %fusion.124 = (f32[1024]{0:T(1024)S(1)}, f32[1024]{0:T(1024)S(1)}, f32[2048,1024]{1,0:T(8,128)}) fusion(bf16[3,256,1024]{2,1,0:T(8,128)(2,1)} %param.11, f32[2048,256]{1,0:T(8,128)} %get-tuple-element.90, f32[256]{0:T(256)} %bitcast.255, f32[256]{0:T(256)S(1)} %bitcast.254, f32[256]{0:T(256)S(1)} %get-tuple-element.86, f32[256]{0:T(256)S(1)} %get-tuple-element.85), kind=kOutput, calls=%fused_computation.206 | convolution fusion | flops 1083176960 | bytes 11022336 | tf_op jit(solution)/shard_map/dot_general | solution.py:80
  61.7 4.2 %all-to-all-start.2 = ((f32[16,1,2048]{2,1,0:T(1,128)}), f32[16,1,2048]{2,1,0:T(1,128)}, u32[]{:S(2)}, u32[]{:S(2)}) async-start(f32[16,1,2048]{2,1,0:T(1,128)} %broadcast_in_dim.20), calls=%async_computation.2 | async-start | bytes 262144 | tf_op jit(solution)/shard_map/all_to_all | solution.py:9
  67.3 6.6 %all-to-all-done.2 = f32[16,1,2048]{2,1,0:T(1,128)} async-done(((f32[16,1,2048]{2,1,0:T(1,128)}), f32[16,1,2048]{2,1,0:T(1,128)}, u32[]{:S(2)}, u32[]{:S(2)}) %all-to-all-start.2) | async-done | bytes 131104 | tf_op jit(solution)/shard_map/all_to_all | solution.py:9
  74.9 5.8 %maximum_convert_fusion.2 = bf16[2048,1024]{1,0:T(8,128)(2,1)S(1)} fusion(f32[2048,1024]{1,0:T(8,128)} %get-tuple-element.91, f32[1024]{0:T(1024)} %bitcast.243, f32[1024]{0:T(1024)} %bitcast.242, f32[1024]{0:T(1024)S(1)} %get-tuple-element.64, f32[1024]{0:T(1024)S(1)} %get-tuple-element.63, bf16[8,256,1024]{2,1,0:T(8,128)(2,1)} %param.8), kind=kLoop, calls=%fused_computation.4 | loop fusion | flops 16777216 | bytes 16793600 | tf_op jit(solution)/shard_map/convert_element_type | solution.py:87
  80.7 4.1 %fusion.128 = (f32[256]{0:T(256)S(1)}, f32[256]{0:T(256)S(1)}, f32[2048,256]{1,0:T(8,128)}) fusion(bf16[2048,1024]{1,0:T(8,128)(2,1)S(1)} %maximum_convert_fusion.2, bf16[3,1024,256]{2,1,0:T(8,128)(2,1)} %param.9), kind=kOutput, calls=%fused_computation.210 | convolution fusion | flops 1075314176 | bytes 6817792 | tf_op jit(solution)/shard_map/dot_general | solution.py:69
  84.8 10.8 %all_to_all.54 = f32[16,1,512]{2,1,0:T(1,128)} all-to-all(f32[16,1,512]{2,1,0:T(1,128)S(1)} %broadcast_in_dim.21), channel_id=1, replica_groups=mesh['img'=8,'slab'=16] {'slab'}, dimensions={0} | all-to-all | bytes 65536 | tf_op jit(solution)/shard_map/all_to_all | solution.py:9
  103.5 4.5 %collective-permute-done.3 = bf16[1,256,256]{2,1,0:T(8,128)(2,1)S(1)} collective-permute-done((bf16[1,256,256]{2,1,0:T(8,128)(2,1)S(1)}, bf16[1,256,256]{2,1,0:T(8,128)(2,1)S(1)}, u32[]{:S(2)}, u32[]{:S(2)}) %collective-permute-start.3) | collective-permute-done | bytes 131104 | tf_op jit(solution)/shard_map/ppermute | solution.py:34
  114.9 15.1 %all_to_all.55 = f32[16,1,512]{2,1,0:T(1,128)} all-to-all(f32[16,1,512]{2,1,0:T(1,128)S(1)} %broadcast_in_dim.22), channel_id=1, replica_groups=mesh['img'=8,'slab'=16] {'slab'}, dimensions={0} | all-to-all | bytes 65536 | tf_op jit(solution)/shard_map/all_to_all | solution.py:9
  130.9 6.4 %fusion.123 = (f32[1024]{0:T(1024)S(1)}, f32[1024]{0:T(1024)S(1)}, f32[2048,1024]{1,0:T(8,128)}) fusion(bf16[3,256,1024]{2,1,0:T(8,128)(2,1)} %param.11, f32[2048,256]{1,0:T(8,128)} %get-tuple-element.93, f32[256]{0:T(256)} %bitcast.253, f32[256]{0:T(256)} %bitcast.252, f32[256]{0:T(256)S(1)} %get-tuple-element.82, f32[256]{0:T(256)S(1)} %get-tuple-element.81), kind=kOutput, calls=%fused_computation.205 | convolution fusion | flops 1083176960 | bytes 11022336 | tf_op jit(solution)/shard_map/dot_general | solution.py:80
  137.3 11.3 %all_to_all.56 = f32[16,1,2048]{2,1,0:T(1,128)} all-to-all(f32[16,1,2048]{2,1,0:T(1,128)S(1)} %broadcast_in_dim.23), channel_id=1, replica_groups=mesh['img'=8,'slab'=16] {'slab'}, dimensions={0} | all-to-all | bytes 262144 | tf_op jit(solution)/shard_map/all_to_all | solution.py:9
  149.6 5.7 %maximum_convert_fusion.1 = bf16[2048,1024]{1,0:T(8,128)(2,1)S(1)} fusion(bf16[2048,1024]{1,0:T(8,128)(2,1)} %copy-done.1, f32[2048,1024]{1,0:T(8,128)} %get-tuple-element.94, f32[1024]{0:T(1024)} %bitcast.241, f32[1024]{0:T(1024)} %bitcast.240, f32[1024]{0:T(1024)S(1)} %get-tuple-element.62, f32[1024]{0:T(1024)S(1)} %get-tuple-element.61), kind=kLoop, calls=%fused_computation.2 | loop fusion | flops 16777216 | bytes 16793600 | tf_op jit(solution)/shard_map/convert_element_type | solution.py:87
  155.4 4.1 %fusion.126 = (f32[256]{0:T(256)S(1)}, f32[256]{0:T(256)S(1)}, f32[2048,256]{1,0:T(8,128)}) fusion(bf16[2048,1024]{1,0:T(8,128)(2,1)S(1)} %maximum_convert_fusion.1, bf16[3,1024,256]{2,1,0:T(8,128)(2,1)} %param.9), kind=kOutput, calls=%fused_computation.208 | convolution fusion | flops 1075314176 | bytes 6817792 | tf_op jit(solution)/shard_map/dot_general | solution.py:69
  159.5 10.8 %all_to_all.57 = f32[16,1,512]{2,1,0:T(1,128)} all-to-all(f32[16,1,512]{2,1,0:T(1,128)S(1)} %broadcast_in_dim.24), channel_id=1, replica_groups=mesh['img'=8,'slab'=16] {'slab'}, dimensions={0} | all-to-all | bytes 65536 | tf_op jit(solution)/shard_map/all_to_all | solution.py:9
  178.2 4.4 %collective-permute-done.5 = bf16[1,256,256]{2,1,0:T(8,128)(2,1)S(1)} collective-permute-done((bf16[1,256,256]{2,1,0:T(8,128)(2,1)S(1)}, bf16[1,256,256]{2,1,0:T(8,128)(2,1)S(1)}, u32[]{:S(2)}, u32[]{:S(2)}) %collective-permute-start.5) | collective-permute-done | bytes 131104 | tf_op jit(solution)/shard_map/ppermute | solution.py:34
  189.5 15.0 %all_to_all.58 = f32[16,1,512]{2,1,0:T(1,128)S(1)} all-to-all(f32[16,1,512]{2,1,0:T(1,128)S(1)} %broadcast_in_dim.25), channel_id=1, replica_groups=mesh['img'=8,'slab'=16] {'slab'}, dimensions={0} | all-to-all | bytes 65536 | tf_op jit(solution)/shard_map/all_to_all | solution.py:9
  204.6 6.4 %fusion.122 = (f32[1024]{0:T(1024)S(1)}, f32[1024]{0:T(1024)S(1)}, f32[2048,1024]{1,0:T(8,128)}) fusion(bf16[3,256,1024]{2,1,0:T(8,128)(2,1)} %param.11, f32[2048,256]{1,0:T(8,128)} %get-tuple-element.96, f32[256]{0:T(256)} %bitcast.251, f32[256]{0:T(256)} %bitcast.250, f32[256]{0:T(256)S(1)} %get-tuple-element.78, f32[256]{0:T(256)S(1)} %get-tuple-element.77), kind=kOutput, calls=%fused_computation.204 | convolution fusion | flops 1083176960 | bytes 11022336 | tf_op jit(solution)/shard_map/dot_general | solution.py:80
  211.0 11.0 %all_to_all.59 = f32[16,1,2048]{2,1,0:T(1,128)S(1)} all-to-all(f32[16,1,2048]{2,1,0:T(1,128)S(1)} %broadcast_in_dim.26), channel_id=1, replica_groups=mesh['img'=8,'slab'=16] {'slab'}, dimensions={0} | all-to-all | bytes 262144 | tf_op jit(solution)/shard_map/all_to_all | solution.py:9
  222.2 7.0 %maximum_convert_fusion = bf16[2048,1024]{1,0:T(8,128)(2,1)} fusion(bf16[2048,1024]{1,0:T(8,128)(2,1)} %copy-done, f32[2048,1024]{1,0:T(8,128)} %get-tuple-element.97, f32[1024]{0:T(1024)S(1)} %bitcast.239, f32[1024]{0:T(1024)S(1)} %bitcast.238, f32[1024]{0:T(1024)S(1)} %get-tuple-element.60, f32[1024]{0:T(1024)S(1)} %get-tuple-element.59), kind=kLoop, calls=%fused_computation | loop fusion | flops 16777216 | bytes 16793600 | tf_op jit(solution)/shard_map/convert_element_type | solution.py:87
  (105 shorter events, 52.7 us)
Async XLA Ops:
  0.0 12.4 %copy-start.3 = (f32[3,2,256]{2,1,0:T(2,128)S(1)}, f32[3,2,256]{2,1,0:T(2,128)}, u32[]{:S(2)}) copy-start(f32[3,2,256]{2,1,0:T(2,128)} %param.12) | copy-start | bytes 18436
  0.0 13.0 %copy-start.4 = (f32[3,2,256]{2,1,0:T(2,128)S(1)}, f32[3,2,256]{2,1,0:T(2,128)}, u32[]{:S(2)}) copy-start(f32[3,2,256]{2,1,0:T(2,128)} %param.13) | copy-start | bytes 18436
  4.2 15.8 %all-to-all-start = ((f32[16,1,512]{2,1,0:T(1,128)}), f32[16,1,512]{2,1,0:T(1,128)S(1)}, u32[]{:S(2)}, u32[]{:S(2)}) async-start(f32[16,1,512]{2,1,0:T(1,128)} %broadcast_in_dim.18), calls=%async_computation | async-start | bytes 65536 | tf_op jit(solution)/shard_map/all_to_all | solution.py:9
  20.5 5.0 %collective-permute-start = (bf16[1,256,256]{2,1,0:T(8,128)(2,1)S(1)}, bf16[1,256,256]{2,1,0:T(8,128)(2,1)S(1)}, u32[]{:S(2)}, u32[]{:S(2)}) collective-permute-start(bf16[1,256,256]{2,1,0:T(8,128)(2,1)S(1)} %get-tuple-element.51), channel_id=1, source_target_pairs={{0,1},{1,2},{2,3},{3,4},{4,5},{5,6},{6,7},{7,8},{8,9},{9,10},{10,1... | collective-permute-start | bytes 393224 | tf_op jit(solution)/shard_map/ppermute | solution.py:31
  23.0 6.9 %collective-permute-start.1 = (bf16[1,256,256]{2,1,0:T(8,128)(2,1)S(1)}, bf16[1,256,256]{2,1,0:T(8,128)(2,1)S(1)}, u32[]{:S(2)}, u32[]{:S(2)}) collective-permute-start(bf16[1,256,256]{2,1,0:T(8,128)(2,1)S(1)} %get-tuple-element.52), channel_id=1, source_target_pairs={{1,0},{2,1},{3,2},{4,3},{5,4},{6,5},{7,6},{8,7},{9,8},{10,9},{11,1... | collective-permute-start | bytes 393224 | tf_op jit(solution)/shard_map/ppermute | solution.py:34
  30.2 2.0 copy-start.2
  38.4 15.4 %all-to-all-start.1 = ((f32[16,1,512]{2,1,0:T(1,128)}), f32[16,1,512]{2,1,0:T(1,128)}, u32[]{:S(2)}, u32[]{:S(2)}) async-start(f32[16,1,512]{2,1,0:T(1,128)} %broadcast_in_dim.19), calls=%async_computation.1 | async-start | bytes 65536 | tf_op jit(solution)/shard_map/all_to_all | solution.py:9
  61.7 12.2 %all-to-all-start.2 = ((f32[16,1,2048]{2,1,0:T(1,128)}), f32[16,1,2048]{2,1,0:T(1,128)}, u32[]{:S(2)}, u32[]{:S(2)}) async-start(f32[16,1,2048]{2,1,0:T(1,128)} %broadcast_in_dim.20), calls=%async_computation.2 | async-start | bytes 262144 | tf_op jit(solution)/shard_map/all_to_all | solution.py:9
  80.7 4.1 %copy-start.1 = (bf16[2048,1024]{1,0:T(8,128)(2,1)}, bf16[2048,1024]{1,0:T(8,128)(2,1)S(1)}, u32[]{:S(2)}) copy-start(bf16[2048,1024]{1,0:T(8,128)(2,1)S(1)} %maximum_convert_fusion.2) | copy-start | bytes 12582916
  80.7 15.8 %copy-start.6 = (f32[1,1,256]{2,1,0:T(1,128)S(1)}, f32[1,1,256]{2,1,0:T(1,128)}, u32[]{:S(2)}) copy-start(f32[1,1,256]{2,1,0:T(1,128)} %get-tuple-element.67) | copy-start | bytes 3076
  98.5 5.0 %collective-permute-start.2 = (bf16[1,256,256]{2,1,0:T(8,128)(2,1)S(1)}, bf16[1,256,256]{2,1,0:T(8,128)(2,1)S(1)}, u32[]{:S(2)}, u32[]{:S(2)}) collective-permute-start(bf16[1,256,256]{2,1,0:T(8,128)(2,1)S(1)} %get-tuple-element.47), channel_id=1, source_target_pairs={{0,1},{1,2},{2,3},{3,4},{4,5},{5,6},{6,7},{7,8},{8,9},{9,10},{10,1... | collective-permute-start | bytes 393224 | tf_op jit(solution)/shard_map/ppermute | solution.py:31
  101.2 6.9 %collective-permute-start.3 = (bf16[1,256,256]{2,1,0:T(8,128)(2,1)S(1)}, bf16[1,256,256]{2,1,0:T(8,128)(2,1)S(1)}, u32[]{:S(2)}, u32[]{:S(2)}) collective-permute-start(bf16[1,256,256]{2,1,0:T(8,128)(2,1)S(1)} %get-tuple-element.48), channel_id=1, source_target_pairs={{1,0},{2,1},{3,2},{4,3},{5,4},{6,5},{7,6},{8,7},{9,8},{10,9},{11,1... | collective-permute-start | bytes 393224 | tf_op jit(solution)/shard_map/ppermute | solution.py:34
  155.4 4.1 %copy-start = (bf16[2048,1024]{1,0:T(8,128)(2,1)}, bf16[2048,1024]{1,0:T(8,128)(2,1)S(1)}, u32[]{:S(2)}) copy-start(bf16[2048,1024]{1,0:T(8,128)(2,1)S(1)} %maximum_convert_fusion.1) | copy-start | bytes 12582916
  155.4 15.8 %copy-start.5 = (f32[1,1,256]{2,1,0:T(1,128)S(1)}, f32[1,1,256]{2,1,0:T(1,128)}, u32[]{:S(2)}) copy-start(f32[1,1,256]{2,1,0:T(1,128)} %get-tuple-element.70) | copy-start | bytes 3076
  173.2 5.0 %collective-permute-start.4 = (bf16[1,256,256]{2,1,0:T(8,128)(2,1)S(1)}, bf16[1,256,256]{2,1,0:T(8,128)(2,1)S(1)}, u32[]{:S(2)}, u32[]{:S(2)}) collective-permute-start(bf16[1,256,256]{2,1,0:T(8,128)(2,1)S(1)} %get-tuple-element.43), channel_id=1, source_target_pairs={{0,1},{1,2},{2,3},{3,4},{4,5},{5,6},{6,7},{7,8},{8,9},{9,10},{10,1... | collective-permute-start | bytes 393224 | tf_op jit(solution)/shard_map/ppermute | solution.py:31
  175.7 6.9 %collective-permute-start.5 = (bf16[1,256,256]{2,1,0:T(8,128)(2,1)S(1)}, bf16[1,256,256]{2,1,0:T(8,128)(2,1)S(1)}, u32[]{:S(2)}, u32[]{:S(2)}) collective-permute-start(bf16[1,256,256]{2,1,0:T(8,128)(2,1)S(1)} %get-tuple-element.44), channel_id=1, source_target_pairs={{1,0},{2,1},{3,2},{4,3},{5,4},{6,5},{7,6},{8,7},{9,8},{10,9},{11,1... | collective-permute-start | bytes 393224 | tf_op jit(solution)/shard_map/ppermute | solution.py:34
where the time goes:
time: 231 us; the launch traced here: 229 us
  blocking collectives  74.1 us (32%)
  matrix products  47.2 us (20%)
  waiting for transfers between devices  35.6 us (15%)
  starting transfers between devices  31.8 us (14%)
  other arithmetic  29.9 us (13%)
  local copies, waits for them, and re-layouts  10 us (4%)
    all_to_all x6, blocking collectives, sent_to_all(): lax.all_to_all(jnp.broadcast_to(x[None], (length, *x.shape)), axis, 0, 0,...  74.1 us
    all_to_all x3, starting transfers between devices, sent_to_all(): lax.all_to_all(jnp.broadcast_to(x[None], (length, *x.shape)), axis, 0, 0,...  20 us
    dot_general x3, matrix products, local(): jnp.dot(inner, w_expand[layer], preferred_element_type=jnp.float32)  19.2 us
    all_to_all x3, waiting for transfers between devices, sent_to_all(): lax.all_to_all(jnp.broadcast_to(x[None], (length, *x.shape)), axis, 0, 0,...  19.2 us
    convert_element_type x3, other arithmetic, local(): jnp.maximum(summed, 0.0).astype(jnp.bfloat16).reshape(rows, width, chans)  18.5 us
    dot_general x27, matrix products, spatial_conv(): jnp.dot(window, taps[3 * down + across], preferred_element_type=jnp.float32)  16.2 us
    ppermute x3, waiting for transfers between devices, with_halo(): lax.ppermute(lax.slice_in_dim(block, 0, width, axis=dim), axis, backward)  13.3 us
    dot_general x3, matrix products, local(): reduced = jnp.dot(flat, w_reduce[layer], preferred_element_type=jnp.float32)  11.8 us
  transfers between devices with their start and end apart: 9, of which 9 were waited for; matrix products, arithmetic and copies ran while one was open for 2% of the time, Pallas kernels for 0%

commit v1 on v0

v1 whole, which is shorter than its diff:
```python
import functools

import jax
import jax.numpy as jnp
from jax import lax
from jax.experimental import pallas as pl
from jax.experimental.pallas import tpu as pltpu
from jax.sharding import PartitionSpec as P

MESH = pl.DeviceIdType.MESH
F32 = jnp.float32
BF16 = jnp.bfloat16


def row_sums(y):
    m, c = y.shape
    y3 = y.reshape(m // 8, 8, c)
    return jnp.sum(y3, axis=0), jnp.sum(y3 * y3, axis=0)


def kernel(
    n, rows, width, chans, mid, layers,
    x_hbm, wr_hbm, ws_hbm, we_hbm, gm_hbm, sm_hbm, go_hbm, so_hbm,
    out_hbm,
    x, wr, ws, we, gm, sm, go, so,
    red, hid, spa, ex,
    halo_out, halo_in, st_out, st_in, se_out, se_in,
    x_sem, w_sem, p_sem, o_sem, hs_sem, hr_sem, ss_sem, sr_sem, es_sem, er_sem,
):
    me = lax.axis_index("slab")
    count = float(rows * width * n)

    def load(src, dst, sem):
        return pltpu.make_async_copy(src, dst, sem)

    def w_copies(layer):
        return (
            load(wr_hbm.at[layer], wr.at[layer], w_sem.at[0, layer]),
            load(ws_hbm.at[layer], ws.at[layer], w_sem.at[1, layer]),
            load(we_hbm.at[layer], we.at[layer], w_sem.at[2, layer]),
        )

    def x_copy(r):
        return load(x_hbm.at[r], x.at[pl.ds(pl.multiple_of(r * width, width), width)], x_sem.at[r])

    params = ((gm_hbm, gm), (sm_hbm, sm), (go_hbm, go), (so_hbm, so))

    w_copies(0)[0].start()
    for r in range(rows):
        x_copy(r).start()
    for i, (a, b) in enumerate(params):
        load(a, b, p_sem.at[i]).start()
    for layer in range(layers):
        for j, c in enumerate(w_copies(layer)):
            if (layer, j) != (0, 0):
                c.start()

    barrier = pltpu.get_barrier_semaphore()
    for d in range(1, n):
        pl.semaphore_signal(
            barrier, inc=1, device_id={"slab": lax.rem(me + d, n)}, device_id_type=MESH
        )

    def block(r):
        return pl.ds(pl.multiple_of(r * width, width), width)

    def send_all(src, dst, slot, send_sem, recv_sem):
        for d in range(1, n):
            pltpu.make_async_remote_copy(
                src_ref=src.at[slot],
                dst_ref=dst.at[slot, d - 1],
                send_sem=send_sem.at[slot],
                recv_sem=recv_sem.at[slot],
                device_id={"slab": lax.rem(me + d, n)},
                device_id_type=MESH,
            ).start()

    def wait_all(dst, slot, sem):
        pltpu.make_async_copy(dst.at[slot], dst.at[slot], sem.at[slot]).wait()

    def pack(s, q):
        return jnp.concatenate(
            [jnp.sum(s, axis=0, keepdims=True), jnp.sum(q, axis=0, keepdims=True)], axis=0
        )

    def coefficients(own, others, gain, shift):
        total = own
        for d in range(n - 1):
            total = total + others[d]
        mean = total[0:1] / count
        var = jnp.maximum(total[1:2] / count - mean * mean, 0.0)
        alpha = lax.rsqrt(var + 1e-05) * gain
        return alpha, shift - mean * alpha

    def reduce_rows(layer, r):
        y = jnp.dot(x[block(r)], wr[layer], preferred_element_type=F32)
        red[block(r)] = y
        return row_sums(y)

    def add2(c, d):
        return c[0] + d[0], c[1] + d[1]

    zero_mid = (jnp.zeros((8, mid), F32), jnp.zeros((8, mid), F32))
    zero_out = (jnp.zeros((8, chans), F32), jnp.zeros((8, chans), F32))

    w_copies(0)[0].wait()

    def first(r, carry):
        x_copy(r).wait()
        return add2(carry, reduce_rows(0, r))

    carry0 = lax.fori_loop(0, rows, first, zero_mid)

    pl.semaphore_wait(barrier, n - 1)
    for i, (a, b) in enumerate(params):
        load(a, b, p_sem.at[i]).wait()

    def halo_copy(layer, side):
        peer = me - 1 if side == 0 else me + 1
        return pltpu.make_async_remote_copy(
            src_ref=halo_out.at[layer, side],
            dst_ref=halo_in.at[layer, 1 - side],
            send_sem=hs_sem.at[layer, side],
            recv_sem=hr_sem.at[layer, 1 - side],
            device_id={"slab": peer},
            device_id_type=MESH,
        )

    has_side = (me > 0, me < n - 1)

    col = lax.broadcasted_iota(jnp.int32, (width, mid), 0)

    def put_hidden(slot, h):
        dst = block(slot)
        hid[dst, mid : 2 * mid] = h.astype(BF16)
        before = jnp.where(col == 0, 0.0, pltpu.roll(h, 1, 0))
        hid[dst, 0:mid] = before.astype(BF16)
        after = jnp.where(col == width - 1, 0.0, pltpu.roll(h, width - 1, 0))
        hid[dst, 2 * mid : 3 * mid] = after.astype(BF16)

    def layer_body(layer, carry):
        own = pack(*carry)
        k = 2 * layer
        st_out[k] = own
        send_all(st_out, st_in, k, ss_sem, sr_sem)
        local_mean = own[0:1] * (1.0 / (rows * width))
        for side in range(2):
            edge = 0 if side == 0 else rows - 1

            @pl.when(has_side[side])
            def _():
                halo_out[layer, side] = (red[block(edge)] - local_mean).astype(BF16)
                halo_copy(layer, side).start()

        wait_all(st_in, k, sr_sem)
        others = [st_in[k, d] for d in range(n - 1)]
        alpha, beta = coefficients(own, others, gm[layer, 0:1], sm[layer, 0:1])

        def hidden_rows(r, c):
            put_hidden(r + 1, jnp.maximum(red[block(r)] * alpha + beta, 0.0))
            return c

        lax.fori_loop(0, rows, hidden_rows, 0)

        w_copies(layer)[1].wait()

        def conv_row(r, carry):
            y = jnp.dot(hid[block(r)], ws[layer, 0], preferred_element_type=F32)
            y = y + jnp.dot(hid[block(r + 1)], ws[layer, 1], preferred_element_type=F32)
            y = y + jnp.dot(hid[block(r + 2)], ws[layer, 2], preferred_element_type=F32)
            spa[block(r)] = y
            return add2(carry, row_sums(y))

        carry = lax.fori_loop(1, rows - 1, conv_row, zero_mid)

        for side in range(2):
            slot = 0 if side == 0 else rows + 1

            @pl.when(has_side[side])
            def _():
                arrived = halo_in.at[layer, side]
                load(arrived, arrived, hr_sem.at[layer, side]).wait()
                their = others[0 if side == 0 else n - 2][0:1] * (1.0 / (rows * width))
                y = halo_in[layer, side].astype(F32) + their
                put_hidden(slot, jnp.maximum(y * alpha + beta, 0.0))

            @pl.when(jnp.logical_not(has_side[side]))
            def _():
                hid[block(slot)] = jnp.zeros((width, 3 * mid), BF16)

        carry = lax.fori_loop(
            0, 2, lambda i, c: conv_row(i * (rows - 1), c), carry
        )

        own = pack(*carry)
        k = 2 * layer + 1
        st_out[k] = own
        send_all(st_out, st_in, k, ss_sem, sr_sem)
        w_copies(layer)[2].wait()
        wait_all(st_in, k, sr_sem)
        others = [st_in[k, d] for d in range(n - 1)]
        alpha, beta = coefficients(own, others, gm[layer, 1:2], sm[layer, 1:2])

        def expand_rows(r, carry):
            inner = jnp.maximum(spa[block(r)] * alpha + beta, 0.0).astype(BF16)
            y = jnp.dot(inner, we[layer], preferred_element_type=F32)
            ex[block(r)] = y
            return add2(carry, row_sums(y))

        carry = lax.fori_loop(0, rows, expand_rows, zero_out)

        own = pack(*carry)
        se_out[layer] = own
        send_all(se_out, se_in, layer, es_sem, er_sem)
        wait_all(se_in, layer, er_sem)
        others = [se_in[layer, d] for d in range(n - 1)]
        alpha, beta = coefficients(own, others, go[pl.ds(layer, 1)], so[pl.ds(layer, 1)])

        def update(r):
            y = ex[block(r)] * alpha + beta + x[block(r)].astype(F32)
            x[block(r)] = jnp.maximum(y, 0.0).astype(BF16)

        def middle():
            w_copies(layer + 1)[0].wait()

            def body(r, carry):
                update(r)
                return add2(carry, reduce_rows(layer + 1, r))

            return lax.fori_loop(0, rows, body, zero_mid)

        def last():
            def body(r, c):
                update(r)
                load(x.at[block(r)], out_hbm.at[r], o_sem.at[r]).start()
                return c

            lax.fori_loop(0, rows, body, 0)
            return zero_mid

        return lax.cond(layer < layers - 1, middle, last)

    lax.fori_loop(0, layers, layer_body, carry0)

    for r in range(rows):
        load(x.at[block(r)], out_hbm.at[r], o_sem.at[r]).wait()
    for layer in range(layers):
        for side in range(2):

            @pl.when(has_side[side])
            def _():
                halo_copy(layer, side).wait_send()

        wait_all(st_in, 2 * layer, ss_sem)
        wait_all(st_in, 2 * layer + 1, ss_sem)
        wait_all(se_in, layer, es_sem)


def solution(mesh):
    n = mesh.shape["slab"]

    def local(x, w_reduce, w_spatial, w_expand, gain_mid, shift_mid, gain_out, shift_out):
        rows, width, chans = x.shape
        layers, _, mid = w_reduce.shape
        taps = w_spatial.reshape(layers, 3, 3 * mid, mid)
        anywhere = pl.BlockSpec(memory_space=pltpu.HBM)
        size = rows * width
        dma = pltpu.SemaphoreType.DMA
        return pl.pallas_call(
            functools.partial(kernel, n, rows, width, chans, mid, layers),
            out_shape=jax.ShapeDtypeStruct(x.shape, BF16),
            in_specs=[anywhere] * 8,
            out_specs=anywhere,
            scratch_shapes=[
                pltpu.VMEM((size, chans), BF16),
                pltpu.VMEM((layers, chans, mid), BF16),
                pltpu.VMEM((layers, 3, 3 * mid, mid), BF16),
                pltpu.VMEM((layers, mid, chans), BF16),
                pltpu.VMEM((layers, 2, mid), F32),
                pltpu.VMEM((layers, 2, mid), F32),
                pltpu.VMEM((layers, chans), F32),
                pltpu.VMEM((layers, chans), F32),
                pltpu.VMEM((size, mid), F32),
                pltpu.VMEM(((rows + 2) * width, 3 * mid), BF16),
                pltpu.VMEM((size, mid), F32),
                pltpu.VMEM((size, chans), F32),
                pltpu.VMEM((layers, 2, width, mid), BF16),
                pltpu.VMEM((layers, 2, width, mid), BF16),
                pltpu.VMEM((2 * layers, 2, mid), F32),
                pltpu.VMEM((2 * layers, n - 1, 2, mid), F32),
                pltpu.VMEM((layers, 2, chans), F32),
                pltpu.VMEM((layers, n - 1, 2, chans), F32),
                dma((rows,)),
                dma((3, layers)),
                dma((4,)),
                dma((rows,)),
                dma((layers, 2)),
                dma((layers, 2)),
                dma((2 * layers,)),
                dma((2 * layers,)),
                dma((layers,)),
                dma((layers,)),
            ],
            compiler_params=pltpu.CompilerParams(
                collective_id=0, has_side_effects=True, vmem_limit_bytes=60 * 1024 * 1024
            ),
            name="blocks",
        )(x, w_reduce, taps, w_expand, gain_mid, shift_mid, gain_out, shift_out)

    placed = (P(("img", "slab"), None, None), P(), P(), P(), P(), P(), P(), P())
    return jax.shard_map(
        local, mesh=mesh, in_specs=placed, out_specs=P(("img", "slab"), None, None), check_vma=False
    )
```

time: 231 us -> 86.6 us (0.37)
  Pallas kernels: 0 us -> 81.8 us
  blocking collectives: 74.1 us -> 0 us
  matrix products: 47.2 us -> 0 us
  waiting for transfers between devices: 35.6 us -> 0 us
  starting transfers between devices: 31.8 us -> 0 us
  other arithmetic: 29.9 us -> 0 us
  local copies, waits for them, and re-layouts: 10 us -> 4.64 us
    pallas_call x0 -> x1, Pallas kernels: none -> 81.8 us  [local(): pl.pallas_call(functools.partial(kernel, n, rows, width, chans, mid, laye...]
    all_to_all x6 -> x0, blocking collectives: 74.1 us -> none  [sent_to_all(): lax.all_to_all(jnp.broadcast_to(x[None], (length, *x.shape)), axis, 0, 0,...]
    dot_general x33 -> x0, matrix products: 47.2 us -> none  [the longest x3 19.2 us: local(): jnp.dot(inner, w_expand[layer], preferred_element_type=jnp.float32)]
    convert_element_type x6 -> x0, other arithmetic: 22.9 us -> none  [the longest x3 18.5 us: local(): jnp.maximum(summed, 0.0).astype(jnp.bfloat16).reshape(rows, width, chans)]
    all_to_all x3 -> x0, starting transfers between devices: 20 us -> none  [sent_to_all(): lax.all_to_all(jnp.broadcast_to(x[None], (length, *x.shape)), axis, 0, 0,...]
    all_to_all x3 -> x0, waiting for transfers between devices: 19.2 us -> none  [sent_to_all(): lax.all_to_all(jnp.broadcast_to(x[None], (length, *x.shape)), axis, 0, 0,...]
    ppermute x6 -> x0, waiting for transfers between devices: 16.5 us -> none  [the longest x3 13.3 us: with_halo(): lax.ppermute(lax.slice_in_dim(block, 0, width, axis=dim), axis, backward)]
    ppermute x6 -> x0, starting transfers between devices: 11.8 us -> none  [the longest x3 7.68 us: with_halo(): lax.ppermute(lax.slice_in_dim(block, block.shape[dim] - width, None, axis...]
  transfers between devices with their start and end apart: 9 -> 0, of which waited for: 9 -> 0; matrix products, arithmetic and copies ran while one was open for 2% -> 0% of each run, Pallas kernels for 0% -> 0%
where the time goes in v1:
time: 86.6 us; the launch traced here: 86.5 us
  Pallas kernels  81.8 us (94%)
  local copies, waits for them, and re-layouts  4.64 us (5%)
    pallas_call x1, Pallas kernels, local(): pl.pallas_call(functools.partial(kernel, n, rows, width, chans, mid, laye...  81.8 us
    unnamed x1, local copies, waits for them, and re-layouts  4.64 us

profile of v1, /device:TPU:0, one launch (start us, length us, event | category | flops | bytes accessed | tf_op | source)
XLA Modules:
  0.0 86.5 jit_solution(17084373241775573701)
XLA Ops:
  0.0 81.8 %blocks.1 = bf16[8,256,1024]{2,1,0:T(8,128)(2,1)} custom-call(bf16[8,256,1024]{2,1,0:T(8,128)(2,1)} %x_hbm.1, bf16[3,1024,256]{2,1,0:T(8,128)(2,1)} %wr_hbm.1, bf16[3,3,768,256]{3,2,1,0:T(8,128)(2,1)} %bitcast.1, bf16[3,256,1024]{2,1,0:T(8,128)(2,1)} %we_hbm.1, f32[3,2,256]{2,1,0:T(2,128)} %gm_hbm.1, f32[3,2,256]{2,1,0:T(2,128)} %sm_hbm.1, ...), custom_call_target="tpu_custom_call" | custom-call | tf_op jit(solution)/shard_map/blocks/pallas_call | solution.py:269
  81.9 4.6 %copy.10 = bf16[8,256,1024]{2,1,0:T(8,128)(2,1)} copy(bf16[8,256,1024]{2,1,0:T(8,128)(2,1)} %blocks.1) | data formatting | bytes 8388608

commit v2 on v1

--- a/solution.py
+++ b/solution.py
@@ -19,13 +19,13 @@
 
 
 def kernel(
-    n, rows, width, chans, mid, layers,
+    n, side_y, rows, width, chans, mid, layers,
     x_hbm, wr_hbm, ws_hbm, we_hbm, gm_hbm, sm_hbm, go_hbm, so_hbm,
-    out_hbm,
-    x, wr, ws, we, gm, sm, go, so,
-    red, hid, spa, ex,
+    ex, x, last_ab,
+    wr, ws, we, gm, sm, go, so,
+    red, hid, spa,
     halo_out, halo_in, st_out, st_in, se_out, se_in,
-    x_sem, w_sem, p_sem, o_sem, hs_sem, hr_sem, ss_sem, sr_sem, es_sem, er_sem,
+    x_sem, w_sem, p_sem, hs_sem, hr_sem, ss_sem, sr_sem, es_sem, er_sem,
 ):
     me = lax.axis_index("slab")
     count = float(rows * width * n)
@@ -62,16 +62,35 @@
         )
 
     def block(r):
+        if isinstance(r, int):
+            return pl.ds(r * width, width)
         return pl.ds(pl.multiple_of(r * width, width), width)
 
+    def slot_of(side):
+        y = lax.rem(me, side_y)
+        if side == 0:
+            wraps = y == 0
+            return jnp.where(wraps, 1 * side_y + 1, 1) - 1
+        wraps = y == side_y - 1
+        return jnp.where(wraps, n - 1, side_y - 1) - 1
+
+    def distance(d):
+        return sum(min(c, side - c) for c, side in ((d // side_y, n // side_y), (d % side_y, side_y)))
+
+    far_first = sorted(range(1, n), key=lambda d: (-distance(d), d))
+
+    def peer(d):
+        z, y = me // side_y, me % side_y
+        return lax.rem(z + d // side_y, n // side_y) * side_y + lax.rem(y + d % side_y, side_y)
+
     def send_all(src, dst, slot, send_sem, recv_sem):
-        for d in range(1, n):
+        for d in far_first:
             pltpu.make_async_remote_copy(
                 src_ref=src.at[slot],
                 dst_ref=dst.at[slot, d - 1],
                 send_sem=send_sem.at[slot],
                 recv_sem=recv_sem.at[slot],
-                device_id={"slab": lax.rem(me + d, n)},
+                device_id={"slab": peer(d)},
                 device_id_type=MESH,
             ).start()
 
@@ -127,6 +146,12 @@
         )
 
     has_side = (me > 0, me < n - 1)
+    for side in range(2):
+
+        @pl.when(jnp.logical_not(has_side[side]))
+        def _():
+            for layer in range(layers):
+                halo_in[layer, side] = jnp.zeros((width, mid), BF16)
 
     col = lax.broadcasted_iota(jnp.int32, (width, mid), 0)
 
@@ -147,50 +172,53 @@
         for side in range(2):
             edge = 0 if side == 0 else rows - 1
 
+            halo_out[layer, side] = (red[block(edge)] - local_mean).astype(BF16)
+
             @pl.when(has_side[side])
             def _():
-                halo_out[layer, side] = (red[block(edge)] - local_mean).astype(BF16)
                 halo_copy(layer, side).start()
 
         wait_all(st_in, k, sr_sem)
         others = [st_in[k, d] for d in range(n - 1)]
         alpha, beta = coefficients(own, others, gm[layer, 0:1], sm[layer, 0:1])
 
-        def hidden_rows(r, c):
+        w_copies(layer)[1].wait()
+
+        def hidden_row(r):
             put_hidden(r + 1, jnp.maximum(red[block(r)] * alpha + beta, 0.0))
-            return c
-
-        lax.fori_loop(0, rows, hidden_rows, 0)
-
-        w_copies(layer)[1].wait()
 
         def conv_row(r, carry):
-            y = jnp.dot(hid[block(r)], ws[layer, 0], preferred_element_type=F32)
-            y = y + jnp.dot(hid[block(r + 1)], ws[layer, 1], preferred_element_type=F32)
-            y = y + jnp.dot(hid[block(r + 2)], ws[layer, 2], preferred_element_type=F32)
+            y = jnp.dot(hid[block(r + 1)], ws[layer, 1], preferred_element_type=F32)
+            if r > 0:
+                y = y + jnp.dot(hid[block(r)], ws[layer, 0], preferred_element_type=F32)
+                y = y + jnp.dot(hid[block(r + 2)], ws[layer, 2], preferred_element_type=F32)
+            else:
+                y = y + jnp.dot(hid[block(r + 2)], ws[layer, 2], preferred_element_type=F32)
+                y = y + jnp.dot(hid[block(r)], ws[layer, 0], preferred_element_type=F32)
             spa[block(r)] = y
             return add2(carry, row_sums(y))
 
-        carry = lax.fori_loop(1, rows - 1, conv_row, zero_mid)
+        hidden_row(0)
+        hidden_row(1)
+        carry = zero_mid
+        for r in range(1, rows - 1):
+            hidden_row(r + 1)
+            carry = conv_row(r, carry)
 
         for side in range(2):
-            slot = 0 if side == 0 else rows + 1
 
             @pl.when(has_side[side])
             def _():
                 arrived = halo_in.at[layer, side]
                 load(arrived, arrived, hr_sem.at[layer, side]).wait()
-                their = others[0 if side == 0 else n - 2][0:1] * (1.0 / (rows * width))
-                y = halo_in[layer, side].astype(F32) + their
-                put_hidden(slot, jnp.maximum(y * alpha + beta, 0.0))
-
-            @pl.when(jnp.logical_not(has_side[side]))
-            def _():
-                hid[block(slot)] = jnp.zeros((width, 3 * mid), BF16)
-
-        carry = lax.fori_loop(
-            0, 2, lambda i, c: conv_row(i * (rows - 1), c), carry
-        )
+
+        for side in range(2):
+            their = st_in[k, slot_of(side)][0:1] * (1.0 / (rows * width))
+            y = halo_in[layer, side].astype(F32) + their
+            h = jnp.maximum(y * alpha + beta, 0.0)
+            put_hidden(0 if side == 0 else rows + 1, jnp.where(has_side[side], h, 0.0))
+        carry = conv_row(0, carry)
+        carry = conv_row(rows - 1, carry)
 
         own = pack(*carry)
         k = 2 * layer + 1
@@ -207,7 +235,9 @@
             ex[block(r)] = y
             return add2(carry, row_sums(y))
 
-        carry = lax.fori_loop(0, rows, expand_rows, zero_out)
+        carry = zero_out
+        for r in range(rows):
+            carry = expand_rows(r, carry)
 
         own = pack(*carry)
         se_out[layer] = own
@@ -222,28 +252,21 @@
 
         def middle():
             w_copies(layer + 1)[0].wait()
-
-            def body(r, carry):
+            carry = zero_mid
+            for r in range(rows):
                 update(r)
-                return add2(carry, reduce_rows(layer + 1, r))
-
-            return lax.fori_loop(0, rows, body, zero_mid)
+                carry = add2(carry, reduce_rows(layer + 1, r))
+            return carry
 
         def last():
-            def body(r, c):
-                update(r)
-                load(x.at[block(r)], out_hbm.at[r], o_sem.at[r]).start()
-                return c
-
-            lax.fori_loop(0, rows, body, 0)
+            last_ab[0:1] = alpha
+            last_ab[1:2] = beta
             return zero_mid
 
         return lax.cond(layer < layers - 1, middle, last)
 
     lax.fori_loop(0, layers, layer_body, carry0)
 
-    for r in range(rows):
-        load(x.at[block(r)], out_hbm.at[r], o_sem.at[r]).wait()
     for layer in range(layers):
         for side in range(2):
 
@@ -256,23 +279,40 @@
         wait_all(se_in, layer, es_sem)
 
 
+def finish(rows, width, ex, x, ab, out_hbm, out, sem):
+    alpha, beta = ab[0:1], ab[1:2]
+    for r in range(rows):
+        at = pl.ds(r * width, width)
+        y = ex[at] * alpha + beta + x[at].astype(F32)
+        out[at] = jnp.maximum(y, 0.0).astype(BF16)
+        pltpu.make_async_copy(out.at[at], out_hbm.at[r], sem.at[r]).start()
+    for r in range(rows):
+        at = pl.ds(r * width, width)
+        pltpu.make_async_copy(out.at[at], out_hbm.at[r], sem.at[r]).wait()
+
+
 def solution(mesh):
     n = mesh.shape["slab"]
+    side_y = 4 if n % 4 == 0 else 1
 
     def local(x, w_reduce, w_spatial, w_expand, gain_mid, shift_mid, gain_out, shift_out):
         rows, width, chans = x.shape
         layers, _, mid = w_reduce.shape
         taps = w_spatial.reshape(layers, 3, 3 * mid, mid)
         anywhere = pl.BlockSpec(memory_space=pltpu.HBM)
+        in_vmem = pl.BlockSpec(memory_space=pltpu.VMEM)
         size = rows * width
         dma = pltpu.SemaphoreType.DMA
-        return pl.pallas_call(
-            functools.partial(kernel, n, rows, width, chans, mid, layers),
-            out_shape=jax.ShapeDtypeStruct(x.shape, BF16),
+        ex, last_x, ab = pl.pallas_call(
+            functools.partial(kernel, n, side_y, rows, width, chans, mid, layers),
+            out_shape=(
+                pltpu.VMEM((size, chans), F32),
+                pltpu.VMEM((size, chans), BF16),
+                pltpu.VMEM((2, chans), F32),
+            ),
             in_specs=[anywhere] * 8,
-            out_specs=anywhere,
+            out_specs=(in_vmem, in_vmem, in_vmem),
             scratch_shapes=[
-                pltpu.VMEM((size, chans), BF16),
                 pltpu.VMEM((layers, chans, mid), BF16),
                 pltpu.VMEM((layers, 3, 3 * mid, mid), BF16),
                 pltpu.VMEM((layers, mid, chans), BF16),
@@ -283,7 +323,6 @@
                 pltpu.VMEM((size, mid), F32),
                 pltpu.VMEM(((rows + 2) * width, 3 * mid), BF16),
                 pltpu.VMEM((size, mid), F32),
-                pltpu.VMEM((size, chans), F32),
                 pltpu.VMEM((layers, 2, width, mid), BF16),
                 pltpu.VMEM((layers, 2, width, mid), BF16),
                 pltpu.VMEM((2 * layers, 2, mid), F32),
@@ -293,7 +332,6 @@
                 dma((rows,)),
                 dma((3, layers)),
                 dma((4,)),
-                dma((rows,)),
                 dma((layers, 2)),
                 dma((layers, 2)),
                 dma((2 * layers,)),
@@ -302,10 +340,19 @@
                 dma((layers,)),
             ],
             compiler_params=pltpu.CompilerParams(
-                collective_id=0, has_side_effects=True, vmem_limit_bytes=60 * 1024 * 1024
+                collective_id=0, has_side_effects=True, vmem_limit_bytes=54_400_000
             ),
             name="blocks",
         )(x, w_reduce, taps, w_expand, gain_mid, shift_mid, gain_out, shift_out)
+        return pl.pallas_call(
+            functools.partial(finish, rows, width),
+            out_shape=jax.ShapeDtypeStruct(x.shape, BF16),
+            in_specs=[in_vmem] * 3,
+            out_specs=anywhere,
+            scratch_shapes=[pltpu.VMEM((size, chans), BF16), dma((rows,))],
+            compiler_params=pltpu.CompilerParams(vmem_limit_bytes=24 * 1024 * 1024),
+            name="finish",
+        )(ex, last_x, ab)
 
     placed = (P(("img", "slab"), None, None), P(), P(), P(), P(), P(), P(), P())
     return jax.shard_map(

time: 86.6 us -> 70.5 us (0.81)
  Pallas kernels: 81.8 us -> 70.4 us
  local copies, waits for them, and re-layouts: 4.64 us -> 0 us
    pallas_call x1 -> x2, Pallas kernels: 81.8 us -> 70.4 us  [the longest x1 68.1 us: local(): pl.pallas_call(functools.partial(kernel, n, side_y, rows, width, chans, m...]
    unnamed x1 -> x0, local copies, waits for them, and re-layouts: 4.64 us -> none
where the time goes in v2:
time: 70.5 us; the launch traced here: 70.4 us
  Pallas kernels  70.4 us (100%)
    pallas_call x1, Pallas kernels, local(): pl.pallas_call(functools.partial(kernel, n, side_y, rows, width, chans, m...  68.1 us
    pallas_call x1, Pallas kernels, local(): pl.pallas_call(functools.partial(finish, rows, width), out_shape=jax.Shap...  2.35 us

profile of v2, /device:TPU:0, one launch (start us, length us, event | category | flops | bytes accessed | tf_op | source)
XLA Modules:
  0.0 70.4 jit_solution(3195751213801049078)
XLA Ops:
  0.0 68.1 %blocks.1 = (f32[2048,1024]{1,0:T(8,128)S(1)}, bf16[2048,1024]{1,0:T(8,128)(2,1)S(1)}, f32[2,1024]{1,0:T(2,128)S(1)}) custom-call(bf16[8,256,1024]{2,1,0:T(8,128)(2,1)} %x_hbm.1, bf16[3,1024,256]{2,1,0:T(8,128)(2,1)} %wr_hbm.1, bf16[3,3,768,256]{3,2,1,0:T(8,128)(2,1)} %bitcast.1, bf16[3,256,1024]{2,1,0:T(8,128)(2,1)} %we_hbm.1, f32[3,2,256]{2,1,0:T(2,128)} %gm_hbm.1, ...), custom_call_target="tpu_custom_call" | custom-call | tf_op jit(solution)/shard_map/blocks/pallas_call | solution.py:306
  68.1 2.4 %finish.1 = bf16[8,256,1024]{2,1,0:T(8,128)(2,1)} custom-call(f32[2048,1024]{1,0:T(8,128)S(1)} %get-tuple-element.8.ex, bf16[2048,1024]{1,0:T(8,128)(2,1)S(1)} %get-tuple-element.9.x, f32[2,1024]{1,0:T(2,128)S(1)} %get-tuple-element.10.ab), custom_call_target="tpu_custom_call" | custom-call | tf_op jit(solution)/shard_map/finish/pallas_call | solution.py:347

commit v3 on v2

--- a/solution.py
+++ b/solution.py
@@ -23,7 +23,7 @@
     x_hbm, wr_hbm, ws_hbm, we_hbm, gm_hbm, sm_hbm, go_hbm, so_hbm,
     ex, x, last_ab,
     wr, ws, we, gm, sm, go, so,
-    red, hid, spa,
+    red, hid, spa, wt, prod,
     halo_out, halo_in, st_out, st_in, se_out, se_in,
     x_sem, w_sem, p_sem, hs_sem, hr_sem, ss_sem, sr_sem, es_sem, er_sem,
 ):
@@ -46,20 +46,18 @@
     params = ((gm_hbm, gm), (sm_hbm, sm), (go_hbm, go), (so_hbm, so))
 
     w_copies(0)[0].start()
-    for r in range(rows):
+    for r in range(2):
         x_copy(r).start()
     for i, (a, b) in enumerate(params):
         load(a, b, p_sem.at[i]).start()
-    for layer in range(layers):
-        for j, c in enumerate(w_copies(layer)):
-            if (layer, j) != (0, 0):
-                c.start()
-
     barrier = pltpu.get_barrier_semaphore()
     for d in range(1, n):
         pl.semaphore_signal(
             barrier, inc=1, device_id={"slab": lax.rem(me + d, n)}, device_id_type=MESH
         )
+    pl.delay(500)
+    for r in range(2, rows):
+        x_copy(r).start()
 
     def block(r):
         if isinstance(r, int):
@@ -124,11 +122,18 @@
 
     w_copies(0)[0].wait()
 
-    def first(r, carry):
-        x_copy(r).wait()
-        return add2(carry, reduce_rows(0, r))
-
-    carry0 = lax.fori_loop(0, rows, first, zero_mid)
+    def first(i, carry):
+        x_copy(2 * i).wait()
+        x_copy(2 * i + 1).wait()
+        carry = add2(carry, reduce_rows(0, 2 * i))
+        return add2(carry, reduce_rows(0, 2 * i + 1))
+
+    carry0 = lax.fori_loop(0, rows // 2, first, zero_mid)
+
+    for layer in range(layers):
+        for j, c in enumerate(w_copies(layer)):
+            if (layer, j) != (0, 0):
+                c.start()
 
     pl.semaphore_wait(barrier, n - 1)
     for i, (a, b) in enumerate(params):
@@ -153,15 +158,17 @@
             for layer in range(layers):
                 halo_in[layer, side] = jnp.zeros((width, mid), BF16)
 
-    col = lax.broadcasted_iota(jnp.int32, (width, mid), 0)
+    row8 = lax.broadcasted_iota(jnp.int32, (8, mid), 0)
 
     def put_hidden(slot, h):
         dst = block(slot)
         hid[dst, mid : 2 * mid] = h.astype(BF16)
-        before = jnp.where(col == 0, 0.0, pltpu.roll(h, 1, 0))
-        hid[dst, 0:mid] = before.astype(BF16)
-        after = jnp.where(col == width - 1, 0.0, pltpu.roll(h, width - 1, 0))
-        hid[dst, 2 * mid : 3 * mid] = after.astype(BF16)
+        before = pltpu.roll(h, 1, 0)
+        edge = jnp.where(row8 == 0, 0.0, before[:8])
+        hid[dst, 0:mid] = jnp.concatenate([edge, before[8:]], axis=0).astype(BF16)
+        after = pltpu.roll(h, width - 1, 0)
+        edge = jnp.where(row8 == 7, 0.0, after[-8:])
+        hid[dst, 2 * mid : 3 * mid] = jnp.concatenate([after[:-8], edge], axis=0).astype(BF16)
 
     def layer_body(layer, carry):
         own = pack(*carry)
@@ -178,32 +185,44 @@
             def _():
                 halo_copy(layer, side).start()
 
+        w_copies(layer)[1].wait()
+
+        @pl.loop(0, 3 * mid // 64)
+        def _(i):
+            at = pl.ds(pl.multiple_of(i * 64, 64), 64)
+            outer = ws[layer, 0, at].astype(F32) + ws[layer, 2, at].astype(F32)
+            inner = ws[layer, 1, at].astype(F32)
+            wt[0, at] = (0.5 * (outer + inner)).astype(BF16)
+            wt[1, at] = (0.5 * (outer - inner)).astype(BF16)
+
         wait_all(st_in, k, sr_sem)
         others = [st_in[k, d] for d in range(n - 1)]
         alpha, beta = coefficients(own, others, gm[layer, 0:1], sm[layer, 0:1])
 
-        w_copies(layer)[1].wait()
-
         def hidden_row(r):
             put_hidden(r + 1, jnp.maximum(red[block(r)] * alpha + beta, 0.0))
 
-        def conv_row(r, carry):
-            y = jnp.dot(hid[block(r + 1)], ws[layer, 1], preferred_element_type=F32)
-            if r > 0:
-                y = y + jnp.dot(hid[block(r)], ws[layer, 0], preferred_element_type=F32)
-                y = y + jnp.dot(hid[block(r + 2)], ws[layer, 2], preferred_element_type=F32)
-            else:
-                y = y + jnp.dot(hid[block(r + 2)], ws[layer, 2], preferred_element_type=F32)
-                y = y + jnp.dot(hid[block(r)], ws[layer, 0], preferred_element_type=F32)
+        def conv_pair(r, carry):
+            d0, d1, d2, d3 = (hid[block(r + i)] for i in range(4))
+            prod[0] = jnp.dot(d1 + d2, wt[0], preferred_element_type=F32)
+            prod[1] = jnp.dot(d2 - d1, wt[1], preferred_element_type=F32)
+            y = jnp.dot(d0 - d2, ws[layer, 0], preferred_element_type=F32)
+            y = y + (prod[0] + prod[1])
             spa[block(r)] = y
+            carry = add2(carry, row_sums(y))
+            y = jnp.dot(d3 - d1, ws[layer, 2], preferred_element_type=F32)
+            y = y + (prod[0] - prod[1])
+            spa[block(r + 1)] = y
             return add2(carry, row_sums(y))
 
+        for r in range(1, 5):
+            hidden_row(r)
+        carry = conv_pair(2, zero_mid)
+        hidden_row(5)
+        hidden_row(6)
+        carry = conv_pair(4, carry)
         hidden_row(0)
-        hidden_row(1)
-        carry = zero_mid
-        for r in range(1, rows - 1):
-            hidden_row(r + 1)
-            carry = conv_row(r, carry)
+        hidden_row(7)
 
         for side in range(2):
 
@@ -217,8 +236,8 @@
             y = halo_in[layer, side].astype(F32) + their
             h = jnp.maximum(y * alpha + beta, 0.0)
             put_hidden(0 if side == 0 else rows + 1, jnp.where(has_side[side], h, 0.0))
-        carry = conv_row(0, carry)
-        carry = conv_row(rows - 1, carry)
+        carry = conv_pair(0, carry)
+        carry = conv_pair(rows - 2, carry)
 
         own = pack(*carry)
         k = 2 * layer + 1
@@ -247,8 +266,8 @@
         alpha, beta = coefficients(own, others, go[pl.ds(layer, 1)], so[pl.ds(layer, 1)])
 
         def update(r):
-            y = ex[block(r)] * alpha + beta + x[block(r)].astype(F32)
-            x[block(r)] = jnp.maximum(y, 0.0).astype(BF16)
+            y = (ex[block(r)] * alpha + beta).astype(BF16) + x[block(r)]
+            x[block(r)] = jnp.maximum(y, jnp.zeros_like(y))
 
         def middle():
             w_copies(layer + 1)[0].wait()
@@ -283,8 +302,8 @@
     alpha, beta = ab[0:1], ab[1:2]
     for r in range(rows):
         at = pl.ds(r * width, width)
-        y = ex[at] * alpha + beta + x[at].astype(F32)
-        out[at] = jnp.maximum(y, 0.0).astype(BF16)
+        y = (ex[at] * alpha + beta).astype(BF16) + x[at]
+        out[at] = jnp.maximum(y, jnp.zeros_like(y))
         pltpu.make_async_copy(out.at[at], out_hbm.at[r], sem.at[r]).start()
     for r in range(rows):
         at = pl.ds(r * width, width)
@@ -323,6 +342,8 @@
                 pltpu.VMEM((size, mid), F32),
                 pltpu.VMEM(((rows + 2) * width, 3 * mid), BF16),
                 pltpu.VMEM((size, mid), F32),
+                pltpu.VMEM((2, 3 * mid, mid), BF16),
+                pltpu.VMEM((2, width, mid), F32),
                 pltpu.VMEM((layers, 2, width, mid), BF16),
                 pltpu.VMEM((layers, 2, width, mid), BF16),
                 pltpu.VMEM((2 * layers, 2, mid), F32),

time: 70.5 us -> 67.3 us (0.955)
  Pallas kernels: 70.4 us -> 67.2 us
    pallas_call x1, Pallas kernels: 68.1 us -> 65 us  [local(): pl.pallas_call(functools.partial(kernel, n, side_y, rows, width, chans, m...]
where the time goes in v3:
time: 67.3 us; the launch traced here: 67.2 us
  Pallas kernels  67.2 us (100%)
    pallas_call x1, Pallas kernels, local(): pl.pallas_call(functools.partial(kernel, n, side_y, rows, width, chans, m...  65 us
    pallas_call x1, Pallas kernels, local(): pl.pallas_call(functools.partial(finish, rows, width), out_shape=jax.Shap...  2.23 us

profile of v3, /device:TPU:0, one launch (start us, length us, event | category | flops | bytes accessed | tf_op | source)
XLA Modules:
  0.0 67.2 jit_solution(16417463915637782136)
XLA Ops:
  0.0 65.0 %blocks.1 = (f32[2048,1024]{1,0:T(8,128)S(1)}, bf16[2048,1024]{1,0:T(8,128)(2,1)S(1)}, f32[2,1024]{1,0:T(2,128)S(1)}) custom-call(bf16[8,256,1024]{2,1,0:T(8,128)(2,1)} %x_hbm.1, bf16[3,1024,256]{2,1,0:T(8,128)(2,1)} %wr_hbm.1, bf16[3,3,768,256]{3,2,1,0:T(8,128)(2,1)} %bitcast.1, bf16[3,256,1024]{2,1,0:T(8,128)(2,1)} %we_hbm.1, f32[3,2,256]{2,1,0:T(2,128)} %gm_hbm.1, ...), custom_call_target="tpu_custom_call" | custom-call | tf_op jit(solution)/shard_map/blocks/pallas_call | solution.py:325
  65.0 2.2 %finish.1 = bf16[8,256,1024]{2,1,0:T(8,128)(2,1)} custom-call(f32[2048,1024]{1,0:T(8,128)S(1)} %get-tuple-element.8.ex, bf16[2048,1024]{1,0:T(8,128)(2,1)S(1)} %get-tuple-element.9.x, f32[2,1024]{1,0:T(2,128)S(1)} %get-tuple-element.10.ab), custom_call_target="tpu_custom_call" | custom-call | tf_op jit(solution)/shard_map/finish/pallas_call | solution.py:368

commit v4 on v3

--- a/solution.py
+++ b/solution.py
@@ -10,6 +10,7 @@
 MESH = pl.DeviceIdType.MESH
 F32 = jnp.float32
 BF16 = jnp.bfloat16
+GROUPS = 2
 
 
 def row_sums(y):
@@ -23,7 +24,7 @@
     x_hbm, wr_hbm, ws_hbm, we_hbm, gm_hbm, sm_hbm, go_hbm, so_hbm,
     ex, x, last_ab,
     wr, ws, we, gm, sm, go, so,
-    red, hid, spa, wt, prod,
+    red, hid, spa, inn, wt, prod,
     halo_out, halo_in, st_out, st_in, se_out, se_in,
     x_sem, w_sem, p_sem, hs_sem, hr_sem, ss_sem, sr_sem, es_sem, er_sem,
 ):
@@ -46,7 +47,8 @@
     params = ((gm_hbm, gm), (sm_hbm, sm), (go_hbm, go), (so_hbm, so))
 
     w_copies(0)[0].start()
-    for r in range(2):
+    early = 3 * rows // 8
+    for r in range(early):
         x_copy(r).start()
     for i, (a, b) in enumerate(params):
         load(a, b, p_sem.at[i]).start()
@@ -55,8 +57,8 @@
         pl.semaphore_signal(
             barrier, inc=1, device_id={"slab": lax.rem(me + d, n)}, device_id_type=MESH
         )
-    pl.delay(500)
-    for r in range(2, rows):
+    pl.delay(300)
+    for r in range(early, rows):
         x_copy(r).start()
 
     def block(r):
@@ -118,17 +120,20 @@
         return c[0] + d[0], c[1] + d[1]
 
     zero_mid = (jnp.zeros((8, mid), F32), jnp.zeros((8, mid), F32))
-    zero_out = (jnp.zeros((8, chans), F32), jnp.zeros((8, chans), F32))
+    cols = chans // GROUPS
+    zero_out = (jnp.zeros((8, cols), F32), jnp.zeros((8, cols), F32))
+
+    def group(g):
+        return pl.ds(g * cols, cols)
 
     w_copies(0)[0].wait()
 
-    def first(i, carry):
-        x_copy(2 * i).wait()
-        x_copy(2 * i + 1).wait()
-        carry = add2(carry, reduce_rows(0, 2 * i))
-        return add2(carry, reduce_rows(0, 2 * i + 1))
-
-    carry0 = lax.fori_loop(0, rows // 2, first, zero_mid)
+    carry0 = zero_mid
+    for part in (range(early), range(early, rows)):
+        for r in part:
+            x_copy(r).wait()
+        for r in part:
+            carry0 = add2(carry0, reduce_rows(0, r))
 
     for layer in range(layers):
         for j, c in enumerate(w_copies(layer)):
@@ -202,27 +207,32 @@
         def hidden_row(r):
             put_hidden(r + 1, jnp.maximum(red[block(r)] * alpha + beta, 0.0))
 
-        def conv_pair(r, carry):
-            d0, d1, d2, d3 = (hid[block(r + i)] for i in range(4))
-            prod[0] = jnp.dot(d1 + d2, wt[0], preferred_element_type=F32)
-            prod[1] = jnp.dot(d2 - d1, wt[1], preferred_element_type=F32)
-            y = jnp.dot(d0 - d2, ws[layer, 0], preferred_element_type=F32)
-            y = y + (prod[0] + prod[1])
+        def finish_row(r, carry, lhs, taps, rest):
+            y = jnp.dot(lhs, taps, preferred_element_type=F32) + rest
             spa[block(r)] = y
-            carry = add2(carry, row_sums(y))
-            y = jnp.dot(d3 - d1, ws[layer, 2], preferred_element_type=F32)
-            y = y + (prod[0] - prod[1])
-            spa[block(r + 1)] = y
             return add2(carry, row_sums(y))
 
-        for r in range(1, 5):
-            hidden_row(r)
-        carry = conv_pair(2, zero_mid)
-        hidden_row(5)
-        hidden_row(6)
-        carry = conv_pair(4, carry)
         hidden_row(0)
-        hidden_row(7)
+        hidden_row(1)
+        carry = zero_mid
+        for r in range(0, rows, 2):
+            a, b = r % 4, r % 4 + 1
+            d1, d2 = hid[block(r + 1)], hid[block(r + 2)]
+            prod[a] = jnp.dot(d1 + d2, wt[0], preferred_element_type=F32)
+            prod[b] = jnp.dot(d2 - d1, wt[1], preferred_element_type=F32)
+            if r + 2 < rows:
+                hidden_row(r + 2)
+                hidden_row(r + 3)
+            both = prod[a] + prod[b]
+            if r > 0:
+                carry = finish_row(r, carry, hid[block(r)] - d2, ws[layer, 0], both)
+            else:
+                spa[block(r)] = both
+            both = prod[a] - prod[b]
+            if r + 2 < rows:
+                carry = finish_row(r + 1, carry, hid[block(r + 3)] - d1, ws[layer, 2], both)
+            else:
+                spa[block(r + 1)] = both
 
         for side in range(2):
 
@@ -236,8 +246,10 @@
             y = halo_in[layer, side].astype(F32) + their
             h = jnp.maximum(y * alpha + beta, 0.0)
             put_hidden(0 if side == 0 else rows + 1, jnp.where(has_side[side], h, 0.0))
-        carry = conv_pair(0, carry)
-        carry = conv_pair(rows - 2, carry)
+        lhs = hid[block(0)] - hid[block(2)]
+        carry = finish_row(0, carry, lhs, ws[layer, 0], spa[block(0)])
+        lhs = hid[block(rows + 1)] - hid[block(rows - 1)]
+        carry = finish_row(rows - 1, carry, lhs, ws[layer, 2], spa[block(rows - 1)])
 
         own = pack(*carry)
         k = 2 * layer + 1
@@ -248,41 +260,64 @@
         others = [st_in[k, d] for d in range(n - 1)]
         alpha, beta = coefficients(own, others, gm[layer, 1:2], sm[layer, 1:2])
 
-        def expand_rows(r, carry):
-            inner = jnp.maximum(spa[block(r)] * alpha + beta, 0.0).astype(BF16)
-            y = jnp.dot(inner, we[layer], preferred_element_type=F32)
-            ex[block(r)] = y
+        def expand_row(r, g, carry):
+            if g == 0:
+                inn[block(r)] = jnp.maximum(spa[block(r)] * alpha + beta, 0.0).astype(BF16)
+            y = jnp.dot(inn[block(r)], we[layer, :, group(g)], preferred_element_type=F32)
+            ex[block(r), group(g)] = y
             return add2(carry, row_sums(y))
 
-        carry = zero_out
-        for r in range(rows):
-            carry = expand_rows(r, carry)
-
-        own = pack(*carry)
-        se_out[layer] = own
-        send_all(se_out, se_in, layer, es_sem, er_sem)
-        wait_all(se_in, layer, er_sem)
-        others = [se_in[layer, d] for d in range(n - 1)]
-        alpha, beta = coefficients(own, others, go[pl.ds(layer, 1)], so[pl.ds(layer, 1)])
-
-        def update(r):
-            y = (ex[block(r)] * alpha + beta).astype(BF16) + x[block(r)]
-            x[block(r)] = jnp.maximum(y, jnp.zeros_like(y))
-
-        def middle():
-            w_copies(layer + 1)[0].wait()
-            carry = zero_mid
+        sums = []
+        for g in range(GROUPS):
+            carry = zero_out
             for r in range(rows):
-                update(r)
-                carry = add2(carry, reduce_rows(layer + 1, r))
-            return carry
-
-        def last():
-            last_ab[0:1] = alpha
-            last_ab[1:2] = beta
-            return zero_mid
-
-        return lax.cond(layer < layers - 1, middle, last)
+                carry = expand_row(r, g, carry)
+            own = pack(*carry)
+            sums.append(own)
+            slot = GROUPS * layer + g
+            se_out[slot] = own
+            send_all(se_out, se_in, slot, es_sem, er_sem)
+
+        carry = zero_mid
+        for g in range(GROUPS):
+            slot = GROUPS * layer + g
+            wait_all(se_in, slot, er_sem)
+            others = [se_in[slot, d] for d in range(n - 1)]
+            at_layer = pl.ds(layer, 1)
+            scale, offset = coefficients(
+                sums[g], others, go[at_layer, group(g)], so[at_layer, group(g)]
+            )
+
+            def update(r):
+                y = (ex[block(r), group(g)] * scale + offset).astype(BF16) + x[block(r), group(g)]
+                x[block(r), group(g)] = jnp.maximum(y, jnp.zeros_like(y))
+
+            def middle():
+                if g == 0:
+                    w_copies(layer + 1)[0].wait()
+                carry = zero_mid
+                for r in range(rows):
+                    update(r)
+                    taps = wr[layer + 1, group(g)]
+                    y = jnp.dot(x[block(r), group(g)], taps, preferred_element_type=F32)
+                    if g > 0:
+                        y = y + red[block(r)]
+                    red[block(r)] = y
+                    if g == GROUPS - 1:
+                        carry = add2(carry, row_sums(y))
+                return carry
+
+            def last():
+                if g < GROUPS - 1:
+                    for r in range(rows):
+                        update(r)
+                else:
+                    last_ab[0:1] = scale
+                    last_ab[1:2] = offset
+                return zero_mid
+
+            carry = lax.cond(layer < layers - 1, middle, last)
+        return carry
 
     lax.fori_loop(0, layers, layer_body, carry0)
 
@@ -295,19 +330,28 @@
 
         wait_all(st_in, 2 * layer, ss_sem)
         wait_all(st_in, 2 * layer + 1, ss_sem)
-        wait_all(se_in, layer, es_sem)
-
-
-def finish(rows, width, ex, x, ab, out_hbm, out, sem):
+        for g in range(GROUPS):
+            wait_all(se_in, GROUPS * layer + g, es_sem)
+
+
+def finish(rows, width, ex, x, ab, out_hbm, out, sem, done_sem):
     alpha, beta = ab[0:1], ab[1:2]
+    cols = ab.shape[1]
+    done = ex.shape[1] - cols
+    ready, left = pl.ds(0, done), pl.ds(done, cols)
+    copies = []
+    for r in range(rows):
+        src = x.at[pl.ds(r * width, width), ready]
+        copies.append(pltpu.make_async_copy(src, out_hbm.at[r, :, ready], done_sem.at[r]))
+        copies[-1].start()
     for r in range(rows):
         at = pl.ds(r * width, width)
-        y = (ex[at] * alpha + beta).astype(BF16) + x[at]
+        y = (ex[at, left] * alpha + beta).astype(BF16) + x[at, left]
         out[at] = jnp.maximum(y, jnp.zeros_like(y))
-        pltpu.make_async_copy(out.at[at], out_hbm.at[r], sem.at[r]).start()
-    for r in range(rows):
-        at = pl.ds(r * width, width)
-        pltpu.make_async_copy(out.at[at], out_hbm.at[r], sem.at[r]).wait()
+        copies.append(pltpu.make_async_copy(out.at[at], out_hbm.at[r, :, left], sem.at[r]))
+        copies[-1].start()
+    for copy in copies:
+        copy.wait()
 
 
 def solution(mesh):
@@ -327,7 +371,7 @@
             out_shape=(
                 pltpu.VMEM((size, chans), F32),
                 pltpu.VMEM((size, chans), BF16),
-                pltpu.VMEM((2, chans), F32),
+                pltpu.VMEM((2, chans // GROUPS), F32),
             ),
             in_specs=[anywhere] * 8,
             out_specs=(in_vmem, in_vmem, in_vmem),
@@ -342,14 +386,15 @@
                 pltpu.VMEM((size, mid), F32),
                 pltpu.VMEM(((rows + 2) * width, 3 * mid), BF16),
                 pltpu.VMEM((size, mid), F32),
+                pltpu.VMEM((size, mid), BF16),
                 pltpu.VMEM((2, 3 * mid, mid), BF16),
-                pltpu.VMEM((2, width, mid), F32),
+                pltpu.VMEM((4, width, mid), F32),
                 pltpu.VMEM((layers, 2, width, mid), BF16),
                 pltpu.VMEM((layers, 2, width, mid), BF16),
                 pltpu.VMEM((2 * layers, 2, mid), F32),
                 pltpu.VMEM((2 * layers, n - 1, 2, mid), F32),
-                pltpu.VMEM((layers, 2, chans), F32),
-                pltpu.VMEM((layers, n - 1, 2, chans), F32),
+                pltpu.VMEM((GROUPS * layers, 2, chans // GROUPS), F32),
+                pltpu.VMEM((GROUPS * layers, n - 1, 2, chans // GROUPS), F32),
                 dma((rows,)),
                 dma((3, layers)),
                 dma((4,)),
@@ -357,8 +402,8 @@
                 dma((layers, 2)),
                 dma((2 * layers,)),
                 dma((2 * layers,)),
-                dma((layers,)),
-                dma((layers,)),
+                dma((GROUPS * layers,)),
+                dma((GROUPS * layers,)),
             ],
             compiler_params=pltpu.CompilerParams(
                 collective_id=0, has_side_effects=True, vmem_limit_bytes=54_400_000
@@ -370,7 +415,7 @@
             out_shape=jax.ShapeDtypeStruct(x.shape, BF16),
             in_specs=[in_vmem] * 3,
             out_specs=anywhere,
-            scratch_shapes=[pltpu.VMEM((size, chans), BF16), dma((rows,))],
+            scratch_shapes=[pltpu.VMEM((size, chans // GROUPS), BF16), dma((rows,)), dma((rows,))],
             compiler_params=pltpu.CompilerParams(vmem_limit_bytes=24 * 1024 * 1024),
             name="finish",
         )(ex, last_x, ab)

time: 67.3 us -> 66.1 us (0.982)
  Pallas kernels: 67.2 us -> 66 us
    pallas_call x1, Pallas kernels: 65 us -> 63.8 us  [local(): pl.pallas_call(functools.partial(kernel, n, side_y, rows, width, chans, m...]
where the time goes in v4:
time: 66.1 us; the launch traced here: 66 us
  Pallas kernels  66 us (100%)
    pallas_call x1, Pallas kernels, local(): pl.pallas_call(functools.partial(kernel, n, side_y, rows, width, chans, m...  63.8 us
    pallas_call x1, Pallas kernels, local(): pl.pallas_call(functools.partial(finish, rows, width), out_shape=jax.Shap...  2.14 us

profile of v4, /device:TPU:0, one launch (start us, length us, event | category | flops | bytes accessed | tf_op | source)
XLA Modules:
  0.0 66.0 jit_solution(215979833503658251)
XLA Ops:
  0.0 63.8 %blocks.1 = (f32[2048,1024]{1,0:T(8,128)S(1)}, bf16[2048,1024]{1,0:T(8,128)(2,1)S(1)}, f32[2,512]{1,0:T(2,128)S(1)}) custom-call(bf16[8,256,1024]{2,1,0:T(8,128)(2,1)} %x_hbm.1, bf16[3,1024,256]{2,1,0:T(8,128)(2,1)} %wr_hbm.1, bf16[3,3,768,256]{3,2,1,0:T(8,128)(2,1)} %bitcast.1, bf16[3,256,1024]{2,1,0:T(8,128)(2,1)} %we_hbm.1, f32[3,2,256]{2,1,0:T(2,128)} %gm_hbm.1, ...), custom_call_target="tpu_custom_call" | custom-call | tf_op jit(solution)/shard_map/blocks/pallas_call | solution.py:369
  63.8 2.1 %finish.1 = bf16[8,256,1024]{2,1,0:T(8,128)(2,1)} custom-call(f32[2048,1024]{1,0:T(8,128)S(1)} %get-tuple-element.8.ex, bf16[2048,1024]{1,0:T(8,128)(2,1)S(1)} %get-tuple-element.9.x, f32[2,512]{1,0:T(2,128)S(1)} %get-tuple-element.10.ab), custom_call_target="tpu_custom_call" | custom-call | tf_op jit(solution)/shard_map/finish/pallas_call | solution.py:413

commit v5 on v4

--- a/solution.py
+++ b/solution.py
@@ -47,7 +47,7 @@
     params = ((gm_hbm, gm), (sm_hbm, sm), (go_hbm, go), (so_hbm, so))
 
     w_copies(0)[0].start()
-    early = 3 * rows // 8
+    early = 4 * rows // 8
     for r in range(early):
         x_copy(r).start()
     for i, (a, b) in enumerate(params):
@@ -57,7 +57,7 @@
         pl.semaphore_signal(
             barrier, inc=1, device_id={"slab": lax.rem(me + d, n)}, device_id_type=MESH
         )
-    pl.delay(300)
+    pl.delay(400)
     for r in range(early, rows):
         x_copy(r).start()
 
@@ -256,6 +256,11 @@
         st_out[k] = own
         send_all(st_out, st_in, k, ss_sem, sr_sem)
         w_copies(layer)[2].wait()
+
+        @pl.loop(0, 13)
+        def _(i):
+            prod[0] = jnp.dot(hid[block(1)], wt[0], preferred_element_type=F32)
+
         wait_all(st_in, k, sr_sem)
         others = [st_in[k, d] for d in range(n - 1)]
         alpha, beta = coefficients(own, others, gm[layer, 1:2], sm[layer, 1:2])
@@ -277,6 +282,11 @@
             slot = GROUPS * layer + g
             se_out[slot] = own
             send_all(se_out, se_in, slot, es_sem, er_sem)
+
+
+        @pl.loop(0, 12)
+        def _(i):
+            prod[0] = jnp.dot(hid[block(1)], wt[0], preferred_element_type=F32)
 
         carry = zero_mid
         for g in range(GROUPS):
@@ -337,18 +347,19 @@
 def finish(rows, width, ex, x, ab, out_hbm, out, sem, done_sem):
     alpha, beta = ab[0:1], ab[1:2]
     cols = ab.shape[1]
-    done = ex.shape[1] - cols
+    done = ex.shape[2] - cols
     ready, left = pl.ds(0, done), pl.ds(done, cols)
     copies = []
-    for r in range(rows):
-        src = x.at[pl.ds(r * width, width), ready]
-        copies.append(pltpu.make_async_copy(src, out_hbm.at[r, :, ready], done_sem.at[r]))
+    half = rows // 2
+    for r in range(0, rows, half):
+        at = pl.ds(r, half)
+        src = x.at[at, :, ready]
+        copies.append(pltpu.make_async_copy(src, out_hbm.at[at, :, ready], done_sem.at[r]))
         copies[-1].start()
     for r in range(rows):
-        at = pl.ds(r * width, width)
-        y = (ex[at, left] * alpha + beta).astype(BF16) + x[at, left]
-        out[at] = jnp.maximum(y, jnp.zeros_like(y))
-        copies.append(pltpu.make_async_copy(out.at[at], out_hbm.at[r, :, left], sem.at[r]))
+        y = (ex[r, :, left] * alpha + beta).astype(BF16) + x[r, :, left]
+        out[r] = jnp.maximum(y, jnp.zeros_like(y))
+        copies.append(pltpu.make_async_copy(out.at[r], out_hbm.at[r, :, left], sem.at[r]))
         copies[-1].start()
     for copy in copies:
         copy.wait()
@@ -415,10 +426,10 @@
             out_shape=jax.ShapeDtypeStruct(x.shape, BF16),
             in_specs=[in_vmem] * 3,
             out_specs=anywhere,
-            scratch_shapes=[pltpu.VMEM((size, chans // GROUPS), BF16), dma((rows,)), dma((rows,))],
+            scratch_shapes=[pltpu.VMEM((rows, width, chans // GROUPS), BF16), dma((rows,)), dma((rows,))],
             compiler_params=pltpu.CompilerParams(vmem_limit_bytes=24 * 1024 * 1024),
             name="finish",
-        )(ex, last_x, ab)
+        )(ex.reshape(rows, width, chans), last_x.reshape(x.shape), ab)
 
     placed = (P(("img", "slab"), None, None), P(), P(), P(), P(), P(), P(), P())
     return jax.shard_map(

time: 66.1 us -> 65.8 us (level)
  no operation moved by 1% of the time
where the time goes in v5:
time: 65.8 us; the launch traced here: 65.7 us
  Pallas kernels  65.7 us (100%)
    pallas_call x1, Pallas kernels, local(): pl.pallas_call(functools.partial(kernel, n, side_y, rows, width, chans, m...  63.5 us
    pallas_call x1, Pallas kernels, local(): pl.pallas_call(functools.partial(finish, rows, width), out_shape=jax.Shap...  2.14 us

profile of v5, /device:TPU:0, one launch (start us, length us, event | category | flops | bytes accessed | tf_op | source)
XLA Modules:
  0.0 65.7 jit_solution(14059010823291133628)
XLA Ops:
  0.0 63.5 %blocks.1 = (f32[2048,1024]{1,0:T(8,128)S(1)}, bf16[2048,1024]{1,0:T(8,128)(2,1)S(1)}, f32[2,512]{1,0:T(2,128)S(1)}) custom-call(bf16[8,256,1024]{2,1,0:T(8,128)(2,1)} %x_hbm.1, bf16[3,1024,256]{2,1,0:T(8,128)(2,1)} %wr_hbm.1, bf16[3,3,768,256]{3,2,1,0:T(8,128)(2,1)} %bitcast.5, bf16[3,256,1024]{2,1,0:T(8,128)(2,1)} %we_hbm.1, f32[3,2,256]{2,1,0:T(2,128)} %gm_hbm.1, ...), custom_call_target="tpu_custom_call" | custom-call | tf_op jit(solution)/shard_map/blocks/pallas_call | solution.py:380
  63.5 2.1 %finish.1 = bf16[8,256,1024]{2,1,0:T(8,128)(2,1)} custom-call(f32[8,256,1024]{2,1,0:T(8,128)S(1)} %bitcast.3, bf16[8,256,1024]{2,1,0:T(8,128)(2,1)S(1)} %bitcast.4, f32[2,512]{1,0:T(2,128)S(1)} %get-tuple-element.10.ab), custom_call_target="tpu_custom_call" | custom-call | tf_op jit(solution)/shard_map/finish/pallas_call | solution.py:424
